TPU v7x, 512 devices: a whole 4x8x8 slice. The times are simulated.
512 devices in a mesh: oct: 8 (over x, z_lo), space: 64 (over z_hi, y, core).
Axes of the slice: x: 4, y: 8, z: 8 (z_hi: 4, z_lo: 2; z = z_hi * 2 + z_lo), core: 2. Of those that a mesh axis runs over, the one named last changes fastest.
Arguments:
- distribution: float32 [1000, 384, 128], P('oct', 'space'), may hold values from 0.05 to 1
- collision_scale: float32 [1, 384, 128], P(None, 'space'), may hold values from 0.4 to 2.5
Outputs:
- advanced: float32 [1000, 384, 128], P('oct', 'space')
All inputs are finite; a program needn't handle non-finite values.
Results may differ from a plain program's by a relative error of at most 0.0003.
Values sent between devices are 32-bit elements; how exact they have to be, the bound alone decides.
A program may use at most 64 MiB of HBM per device.

v0:
```python
import math

import jax
import jax.numpy as jnp
from jax import lax
from jax.sharding import PartitionSpec as P

NV = 10
NZ = 16
STEPS = 3


vel_bound = 4.0
courant = 0.08
time_step = 0.08
base_rate = 0.25
visc_index = 0.81
limiter_eps = 0.01


def from_everyone(value, axis):
    copies = jnp.broadcast_to(value, (lax.axis_size(axis), *value.shape))
    return lax.all_to_all(copies, axis, split_axis=0, concat_axis=0, tiled=True)


def taken_together(value, axis):
    everything = from_everyone(value, axis)
    return jnp.sum(everything, axis=0)


def padded_2(block, sides, width):
    for axis, dim in sides:
        count = lax.axis_size(axis)
        forward = [(i, i + 1) for i in range(count - 1)]
        forward.append((count - 1, 0))
        backward = [(target, source) for source, target in forward]
        low = lax.ppermute(
            lax.slice_in_dim(block, block.shape[dim] - width, None, axis=dim), axis, forward
        )
        high = lax.ppermute(lax.slice_in_dim(block, 0, width, axis=dim), axis, backward)
        block = jnp.concatenate([low, block, high], axis=dim)
    return block


def velocity_parts(vel_index):
    half_count = NV // 2
    per_octant = half_count**3
    octant = vel_index // per_octant
    within = vel_index % per_octant
    spacing = 2.0 * vel_bound / NV
    sign_x = 1.0 - 2.0 * (octant // 4 % 2).astype(jnp.float32)
    sign_y = 1.0 - 2.0 * (octant // 2 % 2).astype(jnp.float32)
    sign_z = 1.0 - 2.0 * (octant % 2).astype(jnp.float32)
    vel_x = sign_x * ((within // (half_count * half_count)).astype(jnp.float32) + 0.5) * spacing
    vel_y = sign_y * ((within // half_count % half_count).astype(jnp.float32) + 0.5) * spacing
    vel_z = sign_z * ((within % half_count).astype(jnp.float32) + 0.5) * spacing
    return (vel_x, vel_y, vel_z)


def moment_weights(vel_x, vel_y, vel_z):
    spacing = 2.0 * vel_bound / NV
    quad = spacing**3 * (2.0 * math.pi) ** (-1.5)
    rows = [
        jnp.ones_like(vel_x),
        vel_x,
        vel_y,
        vel_z,
        vel_x * vel_x + vel_y * vel_y + vel_z * vel_z,
    ]
    return quad * jnp.stack(rows)


def limited(left, right):
    return left * right * (left + right) / (left * left + right * right + limiter_eps)


def divergence_periodic(field, velocity, forward, backward):
    field_next = forward(field)
    slope = limited(field - backward(field), field_next - field)
    flux = jnp.maximum(velocity, 0.0) * (field + 0.5 * slope) + jnp.minimum(velocity, 0.0) * (
        field_next - 0.5 * forward(slope)
    )
    return flux - backward(flux)


def divergence_margin(field, velocity):
    delta = field[:, 1:] - field[:, :-1]
    slope = limited(delta[:, :-1], delta[:, 1:])
    flux = jnp.maximum(velocity, 0.0) * (field[:, 1:-2] + 0.5 * slope[:, :-1]) + jnp.minimum(
        velocity, 0.0
    ) * (field[:, 2:-1] - 0.5 * slope[:, 1:])
    return flux[:, 1:] - flux[:, :-1]


def y_forward(field):
    return jnp.roll(field, -NZ, axis=-1)


def y_backward(field):
    return jnp.roll(field, NZ, axis=-1)


def z_forward(field):
    z_place = lax.iota(jnp.int32, field.shape[-1]) % NZ
    return jnp.where(
        z_place == NZ - 1, jnp.roll(field, NZ - 1, axis=-1), jnp.roll(field, -1, axis=-1)
    )


def z_backward(field):
    z_place = lax.iota(jnp.int32, field.shape[-1]) % NZ
    return jnp.where(z_place == 0, jnp.roll(field, 1 - NZ, axis=-1), jnp.roll(field, 1, axis=-1))


def relax(field, moments, rate_scale, vel_x, vel_y, vel_z):
    moments = moments.reshape(5, 1, field.shape[1], field.shape[2])
    density = moments[0]
    flow_x = moments[1] / density
    flow_y = moments[2] / density
    flow_z = moments[3] / density
    temper = (moments[4] / density - (flow_x * flow_x + flow_y * flow_y + flow_z * flow_z)) / 3.0
    rate = base_rate * rate_scale * density * temper ** (1.0 - visc_index)
    square = (vel_x - flow_x) ** 2 + (vel_y - flow_y) ** 2 + (vel_z - flow_z) ** 2
    equil = density * temper ** (-1.5) * jnp.exp(-square / (2.0 * temper))
    return time_step * rate * (equil - field)


def per_device(distribution, collision_scale):
    vel_count = distribution.shape[0]
    vel_index = lax.axis_index("oct") * vel_count + lax.iota(jnp.int32, vel_count)
    flat_x, flat_y, flat_z = velocity_parts(vel_index)
    weights = moment_weights(flat_x, flat_y, flat_z)
    vel_x = flat_x[:, None, None]
    vel_y = flat_y[:, None, None]
    vel_z = flat_z[:, None, None]
    field = distribution
    for step_id in range(STEPS):
        padded = padded_2(field, (("space", 1),), 2)
        inner = padded[:, 2:-2]
        change = divergence_margin(padded, vel_x)
        change = change + divergence_periodic(inner, vel_y, y_forward, y_backward)
        change = change + divergence_periodic(inner, vel_z, z_forward, z_backward)
        partial_value = jnp.dot(
            weights, inner.reshape(vel_count, -1), precision=lax.Precision.HIGHEST
        )
        moments = taken_together(partial_value, "oct")
        field = (
            inner - courant * change + relax(inner, moments, collision_scale, vel_x, vel_y, vel_z)
        )
    return field


def solution(mesh):
    return jax.shard_map(
        per_device,
        mesh=mesh,
        in_specs=(P("oct", "space", None), P(None, "space", None)),
        out_specs=P("oct", "space", None),
        check_vma=False,
    )
```

profile of v0, /device:TPU:2, one launch (start us, length us, event | category | flops | bytes accessed | tf_op | source)
XLA Modules:
  0.0 83.3 jit_solution(5935779049630549247)
XLA Ops:
  0.1 1.2 %copy.135 = f32[125,6,128]{0,2,1:T(8,128)S(1)} copy(f32[125,6,128]{2,0,1:T(8,128)} %param.2) | data formatting | bytes 768000 | tf_op args[0]
  1.7 0.7 broadcast_in_dim.51
  2.4 9.2 %all-to-all-start = ((f32[8,5,768]{2,1,0:T(8,128)}), f32[8,5,768]{2,1,0:T(8,128)S(1)}, u32[]{:S(2)}, u32[]{:S(2)}) async-start(f32[8,5,768]{2,1,0:T(8,128)} %broadcast_in_dim.51), calls=%async_computation | async-start | bytes 393216 | tf_op jit(solution)/shard_map/all_to_all | solution.py:23
  11.6 1.9 %collective-permute-start = (f32[125,2,128]{0,2,1:T(8,128)S(1)}, f32[125,2,128]{0,2,1:T(8,128)S(1)}, u32[]{:S(2)}, u32[]{:S(2)}) collective-permute-start(f32[125,2,128]{0,2,1:T(8,128)S(1)} %get-tuple-element.81), channel_id=1, source_target_pairs={{0,1},{1,2},{2,3},{3,4},{4,5},{5,6},{6,7},{7,8},{8,9},{9,10},{10,1... | collective-permute-start | bytes 384008 | tf_op jit(solution)/shard_map/ppermute | solution.py:37
  13.6 9.3 %collective-permute-start.1 = (f32[125,2,128]{0,2,1:T(8,128)S(1)}, f32[125,2,128]{0,2,1:T(8,128)S(1)}, u32[]{:S(2)}, u32[]{:S(2)}) collective-permute-start(f32[125,2,128]{0,2,1:T(8,128)S(1)} %get-tuple-element.82), channel_id=1, source_target_pairs={{1,0},{2,1},{3,2},{4,3},{5,4},{6,5},{7,6},{8,7},{9,8},{10,9},{11,1... | collective-permute-start | bytes 384008 | tf_op jit(solution)/shard_map/ppermute | solution.py:40
  24.2 0.9 %copy-done.1 = f32[125,6,128]{0,2,1:T(8,128)S(1)} copy-done((f32[125,6,128]{0,2,1:T(8,128)S(1)}, f32[125,6,128]{0,2,1:T(8,128)}, u32[]{:S(2)}) %copy-start.1) | copy-done | bytes 384024
  28.4 0.9 %fusion.29 = f32[125,6,128]{0,2,1:T(8,128)S(1)} fusion(f32[125,6,128]{0,2,1:T(8,128)S(1)} %copy.135, f32[125,7,128]{0,2,1:T(8,128)S(1)} %fusion.12, f32[125,6,128]{0,2,1:T(8,128)S(1)} %copy-done.11, f32[125,6,112]{0,2,1:T(8,128)S(1)} %slice-done.7, f32[125,6,16]{0,2,1:T(8,128)S(1)} %slice-done.8, f32[125,6,128]{0,2,1:T(8,128)S(1)} %get-tuple-element.67, ...), kind=kLoop, calls=%fused_computation.53 | loop fusion | flops 2400000 | bytes 3476060 | tf_op jit(solution)/shard_map/add | solution.py:148
  30.5 0.9 %copy-done.5 = f32[125,6,128]{0,2,1:T(8,128)S(1)} copy-done((f32[125,6,128]{0,2,1:T(8,128)S(1)}, f32[125,6,128]{0,2,1:T(8,128)}, u32[]{:S(2)}) %copy-start.5) | copy-done | bytes 384024
  32.4 0.7 copy-done.8
  33.2 1.9 %collective-permute-start.2 = (f32[125,2,128]{0,2,1:T(8,128)S(1)}, f32[125,2,128]{0,2,1:T(8,128)S(1)}, u32[]{:S(2)}, u32[]{:S(2)}) collective-permute-start(f32[125,2,128]{0,2,1:T(8,128)S(1)} %get-tuple-element.65), channel_id=1, source_target_pairs={{0,1},{1,2},{2,3},{3,4},{4,5},{5,6},{6,7},{7,8},{8,9},{9,10},{10,1... | collective-permute-start | bytes 384008 | tf_op jit(solution)/shard_map/ppermute | solution.py:37
  35.1 7.9 %collective-permute-start.3 = (f32[125,2,128]{0,2,1:T(8,128)S(1)}, f32[125,2,128]{0,2,1:T(8,128)S(1)}, u32[]{:S(2)}, u32[]{:S(2)}) collective-permute-start(f32[125,2,128]{0,2,1:T(8,128)S(1)} %get-tuple-element.66), channel_id=1, source_target_pairs={{1,0},{2,1},{3,2},{4,3},{5,4},{6,5},{7,6},{8,7},{9,8},{10,9},{11,1... | collective-permute-start | bytes 384008 | tf_op jit(solution)/shard_map/ppermute | solution.py:40
  43.4 0.7 broadcast_in_dim.52
  44.1 5.7 %all-to-all-start.1 = ((f32[8,5,768]{2,1,0:T(8,128)}), f32[8,5,768]{2,1,0:T(8,128)S(1)}, u32[]{:S(2)}, u32[]{:S(2)}) async-start(f32[8,5,768]{2,1,0:T(8,128)} %broadcast_in_dim.52), calls=%async_computation.1 | async-start | bytes 393216 | tf_op jit(solution)/shard_map/all_to_all | solution.py:23
  50.2 4.8 %all-to-all-done.1 = f32[8,5,768]{2,1,0:T(8,128)S(1)} async-done(((f32[8,5,768]{2,1,0:T(8,128)}), f32[8,5,768]{2,1,0:T(8,128)S(1)}, u32[]{:S(2)}, u32[]{:S(2)}) %all-to-all-start.1) | async-done | bytes 122912 | tf_op jit(solution)/shard_map/all_to_all | solution.py:23
  55.2 0.9 %fusion.24 = f32[125,6,128]{0,2,1:T(8,128)S(1)} fusion(f32[125,6,128]{0,2,1:T(8,128)S(1)} %fusion.29, f32[125,7,128]{0,2,1:T(8,128)S(1)} %fusion.7, f32[125,6,128]{0,2,1:T(8,128)S(1)} %copy-done.9, f32[125,6,112]{0,2,1:T(8,128)S(1)} %slice-done.5, f32[125,6,16]{0,2,1:T(8,128)S(1)} %slice-done.6, f32[125,6,128]{0,2,1:T(8,128)S(1)} %get-tuple-element.51, ...), kind=kLoop, calls=%fused_computation.47 | loop fusion | flops 2400000 | bytes 3476060 | tf_op jit(solution)/shard_map/add | solution.py:148
  57.5 0.9 %copy-done.3 = f32[125,6,128]{0,2,1:T(8,128)S(1)} copy-done((f32[125,6,128]{0,2,1:T(8,128)S(1)}, f32[125,6,128]{0,2,1:T(8,128)}, u32[]{:S(2)}) %copy-start.3) | copy-done | bytes 384024
  59.3 0.7 copy-done.6
  60.1 1.9 %collective-permute-start.4 = (f32[125,2,128]{0,2,1:T(8,128)S(1)}, f32[125,2,128]{0,2,1:T(8,128)S(1)}, u32[]{:S(2)}, u32[]{:S(2)}) collective-permute-start(f32[125,2,128]{0,2,1:T(8,128)S(1)} %get-tuple-element.49), channel_id=1, source_target_pairs={{0,1},{1,2},{2,3},{3,4},{4,5},{5,6},{6,7},{7,8},{8,9},{9,10},{10,1... | collective-permute-start | bytes 384008 | tf_op jit(solution)/shard_map/ppermute | solution.py:37
  62.0 7.9 %collective-permute-start.5 = (f32[125,2,128]{0,2,1:T(8,128)S(1)}, f32[125,2,128]{0,2,1:T(8,128)S(1)}, u32[]{:S(2)}, u32[]{:S(2)}) collective-permute-start(f32[125,2,128]{0,2,1:T(8,128)S(1)} %get-tuple-element.50), channel_id=1, source_target_pairs={{1,0},{2,1},{3,2},{4,3},{5,4},{6,5},{7,6},{8,7},{9,8},{10,9},{11,1... | collective-permute-start | bytes 384008 | tf_op jit(solution)/shard_map/ppermute | solution.py:40
  70.3 0.7 broadcast_in_dim.53
  71.0 5.0 %all-to-all-start.2 = ((f32[8,5,768]{2,1,0:T(8,128)}), f32[8,5,768]{2,1,0:T(8,128)S(1)}, u32[]{:S(2)}, u32[]{:S(2)}) async-start(f32[8,5,768]{2,1,0:T(8,128)} %broadcast_in_dim.53), calls=%async_computation.2 | async-start | bytes 393216 | tf_op jit(solution)/shard_map/all_to_all | solution.py:23
  76.5 4.8 %all-to-all-done.2 = f32[8,5,768]{2,1,0:T(8,128)S(1)} async-done(((f32[8,5,768]{2,1,0:T(8,128)}), f32[8,5,768]{2,1,0:T(8,128)S(1)}, u32[]{:S(2)}, u32[]{:S(2)}) %all-to-all-start.2) | async-done | bytes 122912 | tf_op jit(solution)/shard_map/all_to_all | solution.py:23
  81.5 0.9 %fusion.19 = f32[125,6,128]{0,2,1:T(8,128)S(1)} fusion(f32[125,6,128]{0,2,1:T(8,128)S(1)} %fusion.24, f32[125,7,128]{0,2,1:T(8,128)S(1)} %fusion.2, f32[125,6,128]{0,2,1:T(8,128)S(1)} %copy-done.7, f32[125,6,112]{0,2,1:T(8,128)S(1)} %slice-done.3, f32[125,6,16]{0,2,1:T(8,128)S(1)} %slice-done.4, f32[125,6,128]{0,2,1:T(8,128)S(1)} %get-tuple-element.35, ...), kind=kLoop, calls=%fused_computation.41 | loop fusion | flops 2400000 | bytes 3476060 | tf_op jit(solution)/shard_map/add | solution.py:148
  82.4 0.9 %copy.142 = f32[125,6,128]{2,0,1:T(8,128)} copy(f32[125,6,128]{0,2,1:T(8,128)S(1)} %fusion.19) | data formatting | bytes 768000 | tf_op jit(solution)/shard_map/add | solution.py:148
  (140 shorter events, 11.0 us)
Async XLA Ops:
  2.4 24.9 %all-to-all-start = ((f32[8,5,768]{2,1,0:T(8,128)}), f32[8,5,768]{2,1,0:T(8,128)S(1)}, u32[]{:S(2)}, u32[]{:S(2)}) async-start(f32[8,5,768]{2,1,0:T(8,128)} %broadcast_in_dim.51), calls=%async_computation | async-start | bytes 393216 | tf_op jit(solution)/shard_map/all_to_all | solution.py:23
  11.6 15.3 %collective-permute-start = (f32[125,2,128]{0,2,1:T(8,128)S(1)}, f32[125,2,128]{0,2,1:T(8,128)S(1)}, u32[]{:S(2)}, u32[]{:S(2)}) collective-permute-start(f32[125,2,128]{0,2,1:T(8,128)S(1)} %get-tuple-element.81), channel_id=1, source_target_pairs={{0,1},{1,2},{2,3},{3,4},{4,5},{5,6},{6,7},{7,8},{8,9},{9,10},{10,1... | collective-permute-start | bytes 384008 | tf_op jit(solution)/shard_map/ppermute | solution.py:37
  13.6 13.3 %collective-permute-start.1 = (f32[125,2,128]{0,2,1:T(8,128)S(1)}, f32[125,2,128]{0,2,1:T(8,128)S(1)}, u32[]{:S(2)}, u32[]{:S(2)}) collective-permute-start(f32[125,2,128]{0,2,1:T(8,128)S(1)} %get-tuple-element.82), channel_id=1, source_target_pairs={{1,0},{2,1},{3,2},{4,3},{5,4},{6,5},{7,6},{8,7},{9,8},{10,9},{11,1... | collective-permute-start | bytes 384008 | tf_op jit(solution)/shard_map/ppermute | solution.py:40
  24.1 1.0 %copy-start.1 = (f32[125,6,128]{0,2,1:T(8,128)S(1)}, f32[125,6,128]{0,2,1:T(8,128)}, u32[]{:S(2)}) copy-start(f32[125,6,128]{0,2,1:T(8,128)} %copy-done) | copy-start | bytes 1152004
  24.1 1.1 %slice-start = ((f32[125,6,128]{0,2,1:T(8,128)}), f32[125,6,113]{0,2,1:T(8,128)S(1)}, s32[]{:S(2)}) async-start(f32[125,6,128]{0,2,1:T(8,128)} %copy-done), calls=%async_computation.3 | async-start | bytes 737280 | tf_op jit(solution)/shard_map/jit(_roll_static)/slice | solution.py:106
  27.2 1.0 %copy-start.11 = (f32[125,6,128]{0,2,1:T(8,128)S(1)}, f32[125,6,128]{0,2,1:T(8,128)}, u32[]{:S(2)}) copy-start(f32[125,6,128]{0,2,1:T(8,128)} %copy-done.10) | copy-start | bytes 1152004
  27.2 1.0 %slice-start.8 = ((f32[125,6,128]{0,2,1:T(8,128)}), f32[125,6,16]{0,2,1:T(8,128)S(1)}, s32[]{:S(2)}) async-start(f32[125,6,128]{0,2,1:T(8,128)} %copy-done.10), calls=%async_computation.11 | async-start | bytes 98304 | tf_op jit(solution)/shard_map/jit(_roll_static)/slice | solution.py:100
  27.3 1.0 %slice-start.7 = ((f32[125,6,128]{0,2,1:T(8,128)}), f32[125,6,112]{0,2,1:T(8,128)S(1)}, s32[]{:S(2)}) async-start(f32[125,6,128]{0,2,1:T(8,128)} %copy-done.10), calls=%async_computation.10 | async-start | bytes 688128 | tf_op jit(solution)/shard_map/jit(_roll_static)/slice | solution.py:100
  30.5 1.0 %copy-start.5 = (f32[125,6,128]{0,2,1:T(8,128)S(1)}, f32[125,6,128]{0,2,1:T(8,128)}, u32[]{:S(2)}) copy-start(f32[125,6,128]{0,2,1:T(8,128)} %copy-done.4) | copy-start | bytes 1152004
  30.5 1.1 %slice-start.2 = ((f32[125,6,128]{0,2,1:T(8,128)}), f32[125,6,113]{0,2,1:T(8,128)S(1)}, s32[]{:S(2)}) async-start(f32[125,6,128]{0,2,1:T(8,128)} %copy-done.4), calls=%async_computation.5 | async-start | bytes 737280 | tf_op jit(solution)/shard_map/jit(_roll_static)/slice | solution.py:106
  33.2 16.6 %collective-permute-start.2 = (f32[125,2,128]{0,2,1:T(8,128)S(1)}, f32[125,2,128]{0,2,1:T(8,128)S(1)}, u32[]{:S(2)}, u32[]{:S(2)}) collective-permute-start(f32[125,2,128]{0,2,1:T(8,128)S(1)} %get-tuple-element.65), channel_id=1, source_target_pairs={{0,1},{1,2},{2,3},{3,4},{4,5},{5,6},{6,7},{7,8},{8,9},{9,10},{10,1... | collective-permute-start | bytes 384008 | tf_op jit(solution)/shard_map/ppermute | solution.py:37
  35.1 14.7 %collective-permute-start.3 = (f32[125,2,128]{0,2,1:T(8,128)S(1)}, f32[125,2,128]{0,2,1:T(8,128)S(1)}, u32[]{:S(2)}, u32[]{:S(2)}) collective-permute-start(f32[125,2,128]{0,2,1:T(8,128)S(1)} %get-tuple-element.66), channel_id=1, source_target_pairs={{1,0},{2,1},{3,2},{4,3},{5,4},{6,5},{7,6},{8,7},{9,8},{10,9},{11,1... | collective-permute-start | bytes 384008 | tf_op jit(solution)/shard_map/ppermute | solution.py:40
  44.1 10.9 %all-to-all-start.1 = ((f32[8,5,768]{2,1,0:T(8,128)}), f32[8,5,768]{2,1,0:T(8,128)S(1)}, u32[]{:S(2)}, u32[]{:S(2)}) async-start(f32[8,5,768]{2,1,0:T(8,128)} %broadcast_in_dim.52), calls=%async_computation.1 | async-start | bytes 393216 | tf_op jit(solution)/shard_map/all_to_all | solution.py:23
  50.1 5.1 %copy-start.9 = (f32[125,6,128]{0,2,1:T(8,128)S(1)}, f32[125,6,128]{0,2,1:T(8,128)}, u32[]{:S(2)}) copy-start(f32[125,6,128]{0,2,1:T(8,128)} %copy-done.8) | copy-start | bytes 1152004
  50.1 5.1 %slice-start.6 = ((f32[125,6,128]{0,2,1:T(8,128)}), f32[125,6,16]{0,2,1:T(8,128)S(1)}, s32[]{:S(2)}) async-start(f32[125,6,128]{0,2,1:T(8,128)} %copy-done.8), calls=%async_computation.9 | async-start | bytes 98304 | tf_op jit(solution)/shard_map/jit(_roll_static)/slice | solution.py:100
  50.2 5.0 %slice-start.5 = ((f32[125,6,128]{0,2,1:T(8,128)}), f32[125,6,112]{0,2,1:T(8,128)S(1)}, s32[]{:S(2)}) async-start(f32[125,6,128]{0,2,1:T(8,128)} %copy-done.8), calls=%async_computation.8 | async-start | bytes 688128 | tf_op jit(solution)/shard_map/jit(_roll_static)/slice | solution.py:100
  57.4 1.0 %copy-start.3 = (f32[125,6,128]{0,2,1:T(8,128)S(1)}, f32[125,6,128]{0,2,1:T(8,128)}, u32[]{:S(2)}) copy-start(f32[125,6,128]{0,2,1:T(8,128)} %copy-done.2) | copy-start | bytes 1152004
  57.4 1.1 %slice-start.1 = ((f32[125,6,128]{0,2,1:T(8,128)}), f32[125,6,113]{0,2,1:T(8,128)S(1)}, s32[]{:S(2)}) async-start(f32[125,6,128]{0,2,1:T(8,128)} %copy-done.2), calls=%async_computation.4 | async-start | bytes 737280 | tf_op jit(solution)/shard_map/jit(_roll_static)/slice | solution.py:106
  60.1 16.0 %collective-permute-start.4 = (f32[125,2,128]{0,2,1:T(8,128)S(1)}, f32[125,2,128]{0,2,1:T(8,128)S(1)}, u32[]{:S(2)}, u32[]{:S(2)}) collective-permute-start(f32[125,2,128]{0,2,1:T(8,128)S(1)} %get-tuple-element.49), channel_id=1, source_target_pairs={{0,1},{1,2},{2,3},{3,4},{4,5},{5,6},{6,7},{7,8},{8,9},{9,10},{10,1... | collective-permute-start | bytes 384008 | tf_op jit(solution)/shard_map/ppermute | solution.py:37
  62.0 14.0 %collective-permute-start.5 = (f32[125,2,128]{0,2,1:T(8,128)S(1)}, f32[125,2,128]{0,2,1:T(8,128)S(1)}, u32[]{:S(2)}, u32[]{:S(2)}) collective-permute-start(f32[125,2,128]{0,2,1:T(8,128)S(1)} %get-tuple-element.50), channel_id=1, source_target_pairs={{1,0},{2,1},{3,2},{4,3},{5,4},{6,5},{7,6},{8,7},{9,8},{10,9},{11,1... | collective-permute-start | bytes 384008 | tf_op jit(solution)/shard_map/ppermute | solution.py:40
  71.0 10.3 %all-to-all-start.2 = ((f32[8,5,768]{2,1,0:T(8,128)}), f32[8,5,768]{2,1,0:T(8,128)S(1)}, u32[]{:S(2)}, u32[]{:S(2)}) async-start(f32[8,5,768]{2,1,0:T(8,128)} %broadcast_in_dim.53), calls=%async_computation.2 | async-start | bytes 393216 | tf_op jit(solution)/shard_map/all_to_all | solution.py:23
  76.3 5.1 %copy-start.7 = (f32[125,6,128]{0,2,1:T(8,128)S(1)}, f32[125,6,128]{0,2,1:T(8,128)}, u32[]{:S(2)}) copy-start(f32[125,6,128]{0,2,1:T(8,128)} %copy-done.6) | copy-start | bytes 1152004
  76.3 5.1 %slice-start.4 = ((f32[125,6,128]{0,2,1:T(8,128)}), f32[125,6,16]{0,2,1:T(8,128)S(1)}, s32[]{:S(2)}) async-start(f32[125,6,128]{0,2,1:T(8,128)} %copy-done.6), calls=%async_computation.7 | async-start | bytes 98304 | tf_op jit(solution)/shard_map/jit(_roll_static)/slice | solution.py:100
  76.5 5.0 %slice-start.3 = ((f32[125,6,128]{0,2,1:T(8,128)}), f32[125,6,112]{0,2,1:T(8,128)S(1)}, s32[]{:S(2)}) async-start(f32[125,6,128]{0,2,1:T(8,128)} %copy-done.6), calls=%async_computation.6 | async-start | bytes 688128 | tf_op jit(solution)/shard_map/jit(_roll_static)/slice | solution.py:100
  (7 other events, 5.2 us)
where the time goes:
time: 84 us; the launch traced here: 83.3 us
  starting transfers between devices  50.7 us (60%)
  local copies, waits for them, and re-layouts  13.6 us (16%)
  waiting for transfers between devices  9.67 us (12%)
  other arithmetic  7.4 us (9%)
  matrix products  1.14 us (1%)
  between operations  0.84 us (1%)
    ppermute x3, starting transfers between devices, padded_2(): lax.ppermute(lax.slice_in_dim(block, 0, width, axis=dim), axis, backward)  25 us
    all_to_all x3, starting transfers between devices, from_everyone(): return lax.all_to_all(copies, axis, split_axis=0, concat_axis=0, tiled=True)  19.9 us
    all_to_all x3, waiting for transfers between devices, from_everyone(): return lax.all_to_all(copies, axis, split_axis=0, concat_axis=0, tiled=True)  9.65 us
    unnamed x27, local copies, waits for them, and re-layouts  8.82 us
    ppermute x3, starting transfers between devices, padded_2(): lax.ppermute(lax.slice_in_dim(block, block.shape[dim] - width, None, axis...  5.76 us
    add x3, other arithmetic, per_device(): inner - courant * change  2.64 us
    broadcast_in_dim x3, local copies, waits for them, and re-layouts, from_everyone(): copies = jnp.broadcast_to(value, (lax.axis_size(axis), *value.shape))  2.24 us
    add x6, other arithmetic, divergence_periodic(): jnp.maximum(velocity, 0.0) * (field + 0.5 * slope)  2.19 us
  transfers between devices with their start and end apart: 9, of which 2 were waited for; matrix products, arithmetic and copies ran while one was open for 6% of the time, Pallas kernels for 0%

commit v1 on v0

v1 whole, which is shorter than its diff:
```python
import math

import jax
import jax.numpy as jnp
from jax import lax
from jax.experimental import pallas as pl
from jax.experimental.pallas import tpu as pltpu
from jax.sharding import PartitionSpec as P

NV = 10
NZ = 16
STEPS = 3

vel_bound = 4.0
courant = 0.08
time_step = 0.08
base_rate = 0.25
visc_index = 0.81
limiter_eps = 0.01

MESH = pl.DeviceIdType.MESH
HALF = NV // 2
LANES = 128
LAYERS = 6
SPACING = 2.0 * vel_bound / NV
QUAD = SPACING**3 * (2.0 * math.pi) ** (-1.5)
LOG2E = math.log2(math.e)


def digits(v):
    a = jnp.zeros_like(v)
    b = jnp.zeros_like(v)
    for j in range(1, HALF):
        a = a + jnp.where(v >= HALF * HALF * j, 1, 0)
    rest = v - HALF * HALF * a
    for j in range(1, HALF):
        b = b + jnp.where(rest >= HALF * j, 1, 0)
    return a, b, rest - HALF * b


def half_slope(up, mid, down):
    left = mid - up
    right = down - mid
    return (
        0.5 * left * right * (down - up) / (left * left + right * right + limiter_eps)
    )


def kernel(
    n_oct,
    n_space,
    x_ref,
    cs_ref,
    out_ref,
    field,
    trans,
    halo_up,
    halo_down,
    vmag,
    weight,
    part,
    parts_in,
    total,
    param,
    load_sem,
    hs_sem,
    hr_sem,
    ms_sem,
    mr_sem,
):
    octant = lax.axis_index("oct")
    place = lax.axis_index("space")
    neg_x = lax.div(octant, 4)
    neg_y = lax.rem(lax.div(octant, 2), 2)
    neg_z = lax.rem(octant, 2)
    n_vel = x_ref.shape[1]

    def layer(k):
        return k + neg_x * (LAYERS - 1 - 2 * k)

    loads = []
    for k in range(LAYERS):
        copy = pltpu.make_async_copy(x_ref.at[layer(k)], field.at[0, k], load_sem.at[k])
        copy.start()
        loads.append(copy)

    step_x = 1 - 2 * neg_x
    down_place = lax.rem(place + step_x + n_space, n_space)
    up_place = lax.rem(place - step_x + n_space, n_space)

    barrier = pltpu.get_barrier_semaphore()
    for j in range(1, n_oct):
        pl.semaphore_signal(
            barrier,
            inc=1,
            device_id={"oct": lax.rem(octant + j, n_oct)},
            device_id_type=MESH,
        )
    for where in (down_place, up_place):
        pl.semaphore_signal(
            barrier, inc=1, device_id={"space": where}, device_id_type=MESH
        )

    a, b, c = digits(lax.broadcasted_iota(jnp.int32, (n_vel, LANES), 0))
    for d, digit in enumerate((a, b, c)):
        vmag[d] = (digit.astype(jnp.float32) + 0.5) * SPACING
    row = lax.broadcasted_iota(jnp.int32, (32, n_vel), 0)
    a, b, c = digits(lax.broadcasted_iota(jnp.int32, (32, n_vel), 1))
    odd_x, odd_y, odd_z = 2 * a + 1, 2 * b + 1, 2 * c + 1
    square = odd_x * odd_x + odd_y * odd_y + odd_z * odd_z
    sign_x, sign_y, sign_z = 1 - 2 * neg_x, 1 - 2 * neg_y, 1 - 2 * neg_z
    moment = jnp.zeros_like(row)
    for m in range(1, 6):
        moment = moment + jnp.where(row >= LAYERS * m, 1, 0)
    value = jnp.where(moment == 0, 1, 0)
    value = jnp.where(moment == 1, sign_x * odd_x, value)
    value = jnp.where(moment == 2, sign_y * odd_y, value)
    value = jnp.where(moment == 3, sign_z * odd_z, value)
    value = jnp.where(moment == 4, square, value).astype(jnp.float32)
    which = row - LAYERS * moment
    for k in range(LAYERS):
        weight[k] = jnp.where(which == layer(k), value, 0.0).astype(jnp.bfloat16)
    for k in range(LAYERS):
        param[5, k : k + 1, :] = cs_ref[k]

    def edge(at_end):
        lane = lax.broadcasted_iota(jnp.int32, (1, 1, LANES), 2)
        return lax.rem(lane, NZ) == at_end * (NZ - 1)

    first_z = edge(neg_z)
    last_z = edge(1 - neg_z)

    def y_up(v):
        return pltpu.roll(v, NZ + neg_y * (LANES - 2 * NZ), 2)

    def y_down(v):
        return pltpu.roll(v, LANES - NZ - neg_y * (LANES - 2 * NZ), 2)

    def z_up(v):
        near = pltpu.roll(v, 1 + neg_z * (LANES - 2), 2)
        far = pltpu.roll(v, LANES - (NZ - 1) - neg_z * (LANES - 2 * (NZ - 1)), 2)
        return jnp.where(first_z, far, near)

    def z_down(v):
        near = pltpu.roll(v, LANES - 1 - neg_z * (LANES - 2), 2)
        far = pltpu.roll(v, NZ - 1 + neg_z * (LANES - 2 * (NZ - 1)), 2)
        return jnp.where(last_z, far, near)

    chunks = [
        slice(low, min(low + 32, n_vel)) for low in range(0, n_vel, 32)
    ]

    def send_halos(n):
        copies = []
        for i, (src, dst, to) in enumerate(
            (
                (field.at[n, pl.ds(LAYERS - 2, 2)], halo_up.at[n], down_place),
                (field.at[n, 0], halo_down.at[n], up_place),
            )
        ):
            copy = pltpu.make_async_remote_copy(
                src_ref=src,
                dst_ref=dst,
                send_sem=hs_sem.at[n, i],
                recv_sem=hr_sem.at[n, i],
                device_id={"space": to},
                device_id_type=MESH,
            )
            copy.start()
            copies.append(copy)
        return copies

    def send_moments(n):
        acc = jnp.zeros((32, LANES), jnp.float32)
        for k in range(LAYERS):
            rest = field[n, k]
            for piece in range(3):
                term = rest.astype(jnp.bfloat16)
                acc = acc + jnp.dot(
                    weight[k], term, preferred_element_type=jnp.float32
                )
                if piece < 2:
                    rest = rest - term.astype(jnp.float32)
        part[n] = acc
        copies = []
        for j in range(1, n_oct):
            copy = pltpu.make_async_remote_copy(
                src_ref=part.at[n],
                dst_ref=parts_in.at[n, j - 1],
                send_sem=ms_sem.at[n, j - 1],
                recv_sem=mr_sem.at[n, j - 1],
                device_id={"oct": lax.rem(octant + j, n_oct)},
                device_id_type=MESH,
            )
            copy.start()
            copies.append(copy)
        return copies

    def transport_inside(n):
        for rows in chunks:
            f = field[n, :, rows, :]
            speed_x, speed_y, speed_z = vmag[0, rows, :], vmag[1, rows, :], vmag[2, rows, :]
            g = f + half_slope(y_up(f), f, y_down(f))
            change = speed_y * (g - y_up(g))
            g = f + half_slope(z_up(f), f, z_down(f))
            change = change + speed_z * (g - z_up(g))
            t = f - courant * change
            g = f[1:-1] + half_slope(f[:-2], f[1:-1], f[2:])
            moved = (courant * speed_x) * g
            trans[0, rows, :] = t[0]
            trans[1, rows, :] = t[1] - moved[0]
            for k in range(2, LAYERS - 1):
                trans[k, rows, :] = t[k] - moved[k - 1] + moved[k - 2]
            trans[LAYERS - 1, rows, :] = t[LAYERS - 1] + moved[-1]

    def transport_border(n):
        for rows in chunks:
            speed = courant * vmag[0, rows, :]
            up2, up1 = halo_up[n, 0, rows, :], halo_up[n, 1, rows, :]
            f0, f1 = field[n, 0, rows, :], field[n, 1, rows, :]
            f4, f5 = field[n, LAYERS - 2, rows, :], field[n, LAYERS - 1, rows, :]
            down = halo_down[n, rows, :]
            into = speed * (up1 + half_slope(up2, up1, f0))
            first = speed * (f0 + half_slope(up1, f0, f1))
            last = speed * (f5 + half_slope(f4, f5, down))
            trans[0, rows, :] = trans[0, rows, :] + (into - first)
            trans[1, rows, :] = trans[1, rows, :] + first
            trans[LAYERS - 1, rows, :] = trans[LAYERS - 1, rows, :] - last

    def cell_params(n):
        acc = part[n]
        for j in range(n_oct - 1):
            acc = acc + parts_in[n, j]
        total[...] = acc
        s = [total[LAYERS * m : LAYERS * (m + 1), :] for m in range(5)]
        density = QUAD * s[0]
        inv = 1.0 / s[0]
        half = 0.5 * SPACING
        flow_x = half * s[1] * inv
        flow_y = half * s[2] * inv
        flow_z = half * s[3] * inv
        temper = (
            half * half * s[4] * inv
            - (flow_x * flow_x + flow_y * flow_y + flow_z * flow_z)
        ) / 3.0
        log_t = jnp.log(temper)
        rate = (
            (time_step * base_rate)
            * param[5, :LAYERS, :]
            * density
            * jnp.exp((1.0 - visc_index) * log_t)
        )
        param[0, :LAYERS, :] = sign_x.astype(jnp.float32) * flow_x
        param[1, :LAYERS, :] = sign_y.astype(jnp.float32) * flow_y
        param[2, :LAYERS, :] = sign_z.astype(jnp.float32) * flow_z
        param[3, :LAYERS, :] = (-0.5 * LOG2E) / temper
        param[4, :LAYERS, :] = rate * density * jnp.exp(-1.5 * log_t)
        param[6, :LAYERS, :] = rate

    def relaxed(n, k, rows):
        f = field[n, k, rows, :]
        p = [param[i, pl.ds(layer(k), 1), :] for i in range(7)]
        dx = vmag[0, rows, :] - p[0]
        dy = vmag[1, rows, :] - p[1]
        dz = vmag[2, rows, :] - p[2]
        square = dx * dx + dy * dy + dz * dz
        return trans[k, rows, :] + p[4] * jnp.exp2(square * p[3]) - p[6] * f

    for copy in loads:
        copy.wait()
    pl.semaphore_wait(barrier, n_oct + 1)

    sent = []
    halos = send_halos(0)
    for n in range(STEPS):
        moments = send_moments(n)
        sent += halos + moments
        transport_inside(n)
        for copy in halos:
            copy.wait_recv()
        transport_border(n)
        for copy in moments:
            copy.wait_recv()
        cell_params(n)
        if n < STEPS - 1:
            for k in (LAYERS - 2, LAYERS - 1, 0):
                for rows in chunks:
                    field[n + 1, k, rows, :] = relaxed(n, k, rows)
            halos = send_halos(n + 1)
            for k in range(1, LAYERS - 2):
                for rows in chunks:
                    field[n + 1, k, rows, :] = relaxed(n, k, rows)
        else:
            for k in range(LAYERS):
                for rows in chunks:
                    out_ref[layer(k), rows, :] = relaxed(n, k, rows)
    for copy in sent:
        copy.wait_send()


def solution(mesh):
    n_oct, n_space = mesh.shape["oct"], mesh.shape["space"]

    def per_device(distribution, collision_scale):
        x = jnp.transpose(distribution, (1, 0, 2))
        cs = jnp.transpose(collision_scale, (1, 0, 2))
        n_layers, n_vel, lanes = x.shape
        f32 = jnp.float32
        dma = pltpu.SemaphoreType.DMA

        def body(*refs):
            kernel(n_oct, n_space, *refs)

        out = pl.pallas_call(
            body,
            out_shape=jax.ShapeDtypeStruct(x.shape, f32),
            in_specs=[
                pl.BlockSpec(memory_space=pl.ANY),
                pl.BlockSpec(memory_space=pltpu.VMEM),
            ],
            out_specs=pl.BlockSpec(memory_space=pltpu.VMEM),
            scratch_shapes=[
                pltpu.VMEM((STEPS, n_layers, n_vel, lanes), f32),
                pltpu.VMEM((n_layers, n_vel, lanes), f32),
                pltpu.VMEM((STEPS, 2, n_vel, lanes), f32),
                pltpu.VMEM((STEPS, n_vel, lanes), f32),
                pltpu.VMEM((3, n_vel, lanes), f32),
                pltpu.VMEM((n_layers, 32, n_vel), jnp.bfloat16),
                pltpu.VMEM((STEPS, 32, lanes), f32),
                pltpu.VMEM((STEPS, n_oct - 1, 32, lanes), f32),
                pltpu.VMEM((32, lanes), f32),
                pltpu.VMEM((7, 8, lanes), f32),
                dma((n_layers,)),
                dma((STEPS, 2)),
                dma((STEPS, 2)),
                dma((STEPS, n_oct - 1)),
                dma((STEPS, n_oct - 1)),
            ],
            compiler_params=pltpu.CompilerParams(collective_id=0, has_side_effects=True),
        )(x, cs)
        return jnp.transpose(out, (1, 0, 2))

    return jax.shard_map(
        per_device,
        mesh=mesh,
        in_specs=(P("oct", "space", None), P(None, "space", None)),
        out_specs=P("oct", "space", None),
        check_vma=False,
    )
```

time: 84 us -> 36.3 us (0.43)
  starting transfers between devices: 50.7 us -> 0 us
  Pallas kernels: 0 us -> 34.3 us
  local copies, waits for them, and re-layouts: 13.6 us -> 1.77 us
  waiting for transfers between devices: 9.67 us -> 0 us
  other arithmetic: 7.4 us -> 0 us
  matrix products: 1.14 us -> 0 us
    pallas_call x0 -> x1, Pallas kernels: none -> 34.3 us  [per_device(): pl.pallas_call(body, out_shape=jax.ShapeDtypeStruct(x.shape, f32), in_spe...]
    ppermute x6 -> x0, starting transfers between devices: 30.8 us -> none  [the longest x3 25 us: padded_2(): lax.ppermute(lax.slice_in_dim(block, 0, width, axis=dim), axis, backward)]
    all_to_all x3 -> x0, starting transfers between devices: 19.9 us -> none  [from_everyone(): return lax.all_to_all(copies, axis, split_axis=0, concat_axis=0, tiled=True)]
    all_to_all x3 -> x0, waiting for transfers between devices: 9.65 us -> none  [from_everyone(): return lax.all_to_all(copies, axis, split_axis=0, concat_axis=0, tiled=True)]
    unnamed x27 -> x1, local copies, waits for them, and re-layouts: 8.82 us -> 1.77 us
    add x13 -> x0, other arithmetic: 5.23 us -> none  [the longest x3 2.64 us: per_device(): inner - courant * change]
    broadcast_in_dim x3 -> x0, local copies, waits for them, and re-layouts: 2.24 us -> none  [from_everyone(): copies = jnp.broadcast_to(value, (lax.axis_size(axis), *value.shape))]
    slice x66 -> x0, local copies, waits for them, and re-layouts: 1.59 us -> none  [the longest x15 0.54 us: z_forward(): jnp.roll(field, NZ - 1, axis=-1)]
  transfers between devices with their start and end apart: 9 -> 0, of which waited for: 2 -> 0; matrix products, arithmetic and copies ran while one was open for 6% -> 0% of each run, Pallas kernels for 0% -> 0%
where the time goes in v1:
time: 36.3 us; the launch traced here: 36 us
  Pallas kernels  34.3 us (94%)
  local copies, waits for them, and re-layouts  1.77 us (5%)
    pallas_call x1, Pallas kernels, per_device(): pl.pallas_call(body, out_shape=jax.ShapeDtypeStruct(x.shape, f32), in_spe...  34.3 us
    unnamed x1, local copies, waits for them, and re-layouts  1.77 us

profile of v1, /device:TPU:2, one launch (start us, length us, event | category | flops | bytes accessed | tf_op | source)
XLA Modules:
  0.0 36.0 jit_solution(2347962635622058228)
XLA Ops:
  0.0 34.3 %shard_map.28 = f32[6,125,128]{2,1,0:T(8,128)} custom-call(f32[6,125,128]{2,1,0:T(8,128)} %bitcast.4, f32[6,1,128]{2,1,0:T(1,128)} %bitcast.5), custom_call_target="tpu_custom_call" | custom-call | tf_op jit(solution)/shard_map/pallas_call | solution.py:314
  34.3 1.8 %copy.4 = f32[125,6,128]{2,0,1:T(8,128)} copy(f32[125,6,128]{2,0,1:T(8,128)} %bitcast.3) | data formatting | bytes 768000

commit v2 on v1

--- a/solution.py
+++ b/solution.py
@@ -150,29 +150,26 @@
         slice(low, min(low + 32, n_vel)) for low in range(0, n_vel, 32)
     ]
 
-    def send_halos(n):
-        copies = []
-        for i, (src, dst, to) in enumerate(
-            (
-                (field.at[n, pl.ds(LAYERS - 2, 2)], halo_up.at[n], down_place),
-                (field.at[n, 0], halo_down.at[n], up_place),
-            )
-        ):
-            copy = pltpu.make_async_remote_copy(
-                src_ref=src,
-                dst_ref=dst,
-                send_sem=hs_sem.at[n, i],
-                recv_sem=hr_sem.at[n, i],
-                device_id={"space": to},
-                device_id_type=MESH,
-            )
-            copy.start()
-            copies.append(copy)
-        return copies
-
-    def send_moments(n):
+    def send_layer(n, i):
+        src, dst, to = (
+            (LAYERS - 2, halo_up.at[n, 0], down_place),
+            (LAYERS - 1, halo_up.at[n, 1], down_place),
+            (0, halo_down.at[n], up_place),
+        )[i]
+        copy = pltpu.make_async_remote_copy(
+            src_ref=field.at[n, src],
+            dst_ref=dst,
+            send_sem=hs_sem.at[n, i],
+            recv_sem=hr_sem.at[n, i],
+            device_id={"space": to},
+            device_id_type=MESH,
+        )
+        copy.start()
+        return copy
+
+    def moments_of(n, layers):
         acc = jnp.zeros((32, LANES), jnp.float32)
-        for k in range(LAYERS):
+        for k in layers:
             rest = field[n, k]
             for piece in range(3):
                 term = rest.astype(jnp.bfloat16)
@@ -181,6 +178,9 @@
                 )
                 if piece < 2:
                     rest = rest - term.astype(jnp.float32)
+        return acc
+
+    def send_moments(n, acc):
         part[n] = acc
         copies = []
         for j in range(1, n_oct):
@@ -213,7 +213,13 @@
                 trans[k, rows, :] = t[k] - moved[k - 1] + moved[k - 2]
             trans[LAYERS - 1, rows, :] = t[LAYERS - 1] + moved[-1]
 
-    def transport_border(n):
+    def put(n, k, rows, new):
+        if n < STEPS - 1:
+            field[n + 1, k, rows, :] = new
+        else:
+            out_ref[layer(k), rows, :] = new
+
+    def finish_border(n):
         for rows in chunks:
             speed = courant * vmag[0, rows, :]
             up2, up1 = halo_up[n, 0, rows, :], halo_up[n, 1, rows, :]
@@ -223,9 +229,9 @@
             into = speed * (up1 + half_slope(up2, up1, f0))
             first = speed * (f0 + half_slope(up1, f0, f1))
             last = speed * (f5 + half_slope(f4, f5, down))
-            trans[0, rows, :] = trans[0, rows, :] + (into - first)
-            trans[1, rows, :] = trans[1, rows, :] + first
-            trans[LAYERS - 1, rows, :] = trans[LAYERS - 1, rows, :] - last
+            put(n, LAYERS - 1, rows, trans[LAYERS - 1, rows, :] - last)
+            put(n, 0, rows, trans[0, rows, :] + (into - first))
+            put(n, 1, rows, trans[1, rows, :] + first)
 
     def cell_params(n):
         acc = part[n]
@@ -270,30 +276,35 @@
         copy.wait()
     pl.semaphore_wait(barrier, n_oct + 1)
 
-    sent = []
-    halos = send_halos(0)
+    border = (0, 1, LAYERS - 1)
+    inside = tuple(range(2, LAYERS - 1))
+    halos = [send_layer(0, i) for i in (1, 0, 2)]
+    moments = send_moments(0, moments_of(0, range(LAYERS)))
+    sent = halos + moments
     for n in range(STEPS):
-        moments = send_moments(n)
-        sent += halos + moments
+        more = n < STEPS - 1
         transport_inside(n)
-        for copy in halos:
-            copy.wait_recv()
-        transport_border(n)
         for copy in moments:
             copy.wait_recv()
         cell_params(n)
-        if n < STEPS - 1:
-            for k in (LAYERS - 2, LAYERS - 1, 0):
-                for rows in chunks:
-                    field[n + 1, k, rows, :] = relaxed(n, k, rows)
-            halos = send_halos(n + 1)
-            for k in range(1, LAYERS - 2):
-                for rows in chunks:
-                    field[n + 1, k, rows, :] = relaxed(n, k, rows)
-        else:
-            for k in range(LAYERS):
-                for rows in chunks:
-                    out_ref[layer(k), rows, :] = relaxed(n, k, rows)
+        early = []
+        for k in reversed(inside):
+            for rows in chunks:
+                put(n, k, rows, relaxed(n, k, rows))
+            if more and k == LAYERS - 2:
+                early.append(send_layer(n + 1, 0))
+        for k in border:
+            for rows in chunks:
+                trans[k, rows, :] = relaxed(n, k, rows)
+        if more:
+            acc = moments_of(n + 1, inside)
+        for copy in halos:
+            copy.wait_recv()
+        finish_border(n)
+        if more:
+            halos = early + [send_layer(n + 1, i) for i in (1, 2)]
+            moments = send_moments(n + 1, acc + moments_of(n + 1, border))
+            sent += halos + moments
     for copy in sent:
         copy.wait_send()
 
@@ -315,7 +326,7 @@
             body,
             out_shape=jax.ShapeDtypeStruct(x.shape, f32),
             in_specs=[
-                pl.BlockSpec(memory_space=pl.ANY),
+                pl.BlockSpec(memory_space=pltpu.HBM),
                 pl.BlockSpec(memory_space=pltpu.VMEM),
             ],
             out_specs=pl.BlockSpec(memory_space=pltpu.VMEM),
@@ -331,12 +342,14 @@
                 pltpu.VMEM((32, lanes), f32),
                 pltpu.VMEM((7, 8, lanes), f32),
                 dma((n_layers,)),
-                dma((STEPS, 2)),
-                dma((STEPS, 2)),
+                dma((STEPS, 3)),
+                dma((STEPS, 3)),
                 dma((STEPS, n_oct - 1)),
                 dma((STEPS, n_oct - 1)),
             ],
-            compiler_params=pltpu.CompilerParams(collective_id=0, has_side_effects=True),
+            compiler_params=pltpu.CompilerParams(
+                collective_id=0, has_side_effects=True, vmem_limit_bytes=8 * 2**20
+            ),
         )(x, cs)
         return jnp.transpose(out, (1, 0, 2))
 

time: 36.3 us -> 35.1 us (0.967)
  Pallas kernels: 34.3 us -> 32.5 us
  local copies, waits for them, and re-layouts: 1.77 us -> 2.43 us
    pallas_call x1, Pallas kernels: 34.3 us -> 32.5 us  [per_device(): pl.pallas_call(body, out_shape=jax.ShapeDtypeStruct(x.shape, f32), in_spe...]
    unnamed x1 -> x5, local copies, waits for them, and re-layouts: 1.77 us -> 2.43 us
where the time goes in v2:
time: 35.1 us; the launch traced here: 34.9 us
  Pallas kernels  32.5 us (93%)
  local copies, waits for them, and re-layouts  2.43 us (7%)
    pallas_call x1, Pallas kernels, per_device(): pl.pallas_call(body, out_shape=jax.ShapeDtypeStruct(x.shape, f32), in_spe...  32.5 us
    unnamed x5, local copies, waits for them, and re-layouts  2.43 us

profile of v2, /device:TPU:2, one launch (start us, length us, event | category | flops | bytes accessed | tf_op | source)
XLA Modules:
  0.0 34.9 jit_solution(3511232586304962047)
XLA Ops:
  0.0 0.0 copy-start.1
  0.0 0.7 %copy-done.1 = f32[1,6,128]{2,0,1:T(1,128)S(1)} copy-done((f32[1,6,128]{2,0,1:T(1,128)S(1)}, f32[1,6,128]{2,0,1:T(1,128)}, u32[]{:S(2)}) %copy-start.1) | copy-done | bytes 3096
  0.7 0.0 copy-start
  0.7 1.0 %copy-done = f32[125,6,128]{2,0,1:T(8,128)S(1)} copy-done((f32[125,6,128]{2,0,1:T(8,128)S(1)}, f32[125,6,128]{2,0,1:T(8,128)}, u32[]{:S(2)}) %copy-start) | copy-done | bytes 384024
  1.7 32.5 %shard_map.28 = f32[6,125,128]{2,1,0:T(8,128)S(1)} custom-call(f32[6,125,128]{2,1,0:T(8,128)S(1)} %bitcast.4, f32[6,1,128]{2,1,0:T(1,128)S(1)} %bitcast.5), custom_call_target="tpu_custom_call" | custom-call | tf_op jit(solution)/shard_map/pallas_call | solution.py:325
  34.2 0.7 %copy.4 = f32[125,6,128]{2,0,1:T(8,128)} copy(f32[125,6,128]{2,0,1:T(8,128)S(1)} %bitcast.3) | data formatting | bytes 768000
Async XLA Ops:
  0.0 0.7 %copy-start.1 = (f32[1,6,128]{2,0,1:T(1,128)S(1)}, f32[1,6,128]{2,0,1:T(1,128)}, u32[]{:S(2)}) copy-start(f32[1,6,128]{2,0,1:T(1,128)} %param.3) | copy-start | bytes 9220
  0.7 1.0 %copy-start = (f32[125,6,128]{2,0,1:T(8,128)S(1)}, f32[125,6,128]{2,0,1:T(8,128)}, u32[]{:S(2)}) copy-start(f32[125,6,128]{2,0,1:T(8,128)} %param.2) | copy-start | bytes 1152004

commit v3 on v2

--- a/solution.py
+++ b/solution.py
@@ -62,6 +62,7 @@
     parts_in,
     total,
     param,
+    scale,
     load_sem,
     hs_sem,
     hr_sem,
@@ -83,6 +84,10 @@
         copy = pltpu.make_async_copy(x_ref.at[layer(k)], field.at[0, k], load_sem.at[k])
         copy.start()
         loads.append(copy)
+
+    copy = pltpu.make_async_copy(cs_ref, scale, load_sem.at[LAYERS])
+    copy.start()
+    loads.append(copy)
 
     step_x = 1 - 2 * neg_x
     down_place = lax.rem(place + step_x + n_space, n_space)
@@ -120,8 +125,6 @@
     which = row - LAYERS * moment
     for k in range(LAYERS):
         weight[k] = jnp.where(which == layer(k), value, 0.0).astype(jnp.bfloat16)
-    for k in range(LAYERS):
-        param[5, k : k + 1, :] = cs_ref[k]
 
     def edge(at_end):
         lane = lax.broadcasted_iota(jnp.int32, (1, 1, LANES), 2)
@@ -274,6 +277,8 @@
 
     for copy in loads:
         copy.wait()
+    for k in range(LAYERS):
+        param[5, k : k + 1, :] = scale[k]
     pl.semaphore_wait(barrier, n_oct + 1)
 
     border = (0, 1, LAYERS - 1)
@@ -315,6 +320,8 @@
     def per_device(distribution, collision_scale):
         x = jnp.transpose(distribution, (1, 0, 2))
         cs = jnp.transpose(collision_scale, (1, 0, 2))
+        x = pltpu.with_memory_space_constraint(x, pltpu.HBM)
+        cs = pltpu.with_memory_space_constraint(cs, pltpu.HBM)
         n_layers, n_vel, lanes = x.shape
         f32 = jnp.float32
         dma = pltpu.SemaphoreType.DMA
@@ -327,7 +334,7 @@
             out_shape=jax.ShapeDtypeStruct(x.shape, f32),
             in_specs=[
                 pl.BlockSpec(memory_space=pltpu.HBM),
-                pl.BlockSpec(memory_space=pltpu.VMEM),
+                pl.BlockSpec(memory_space=pltpu.HBM),
             ],
             out_specs=pl.BlockSpec(memory_space=pltpu.VMEM),
             scratch_shapes=[
@@ -341,7 +348,8 @@
                 pltpu.VMEM((STEPS, n_oct - 1, 32, lanes), f32),
                 pltpu.VMEM((32, lanes), f32),
                 pltpu.VMEM((7, 8, lanes), f32),
-                dma((n_layers,)),
+                pltpu.VMEM((n_layers, 1, lanes), f32),
+                dma((n_layers + 1,)),
                 dma((STEPS, 3)),
                 dma((STEPS, 3)),
                 dma((STEPS, n_oct - 1)),

time: 35.1 us -> 33 us (0.940)
  local copies, waits for them, and re-layouts: 2.43 us -> 0.75 us
  Pallas kernels: 32.5 us -> 32 us
    unnamed x5 -> x1, local copies, waits for them, and re-layouts: 2.43 us -> 0.75 us
    pallas_call x1, Pallas kernels: 32.5 us -> 32 us  [per_device(): pl.pallas_call(body, out_shape=jax.ShapeDtypeStruct(x.shape, f32), in_spe...]
where the time goes in v3:
time: 33 us; the launch traced here: 32.8 us
  Pallas kernels  32 us (97%)
  local copies, waits for them, and re-layouts  0.75 us (2%)
    pallas_call x1, Pallas kernels, per_device(): pl.pallas_call(body, out_shape=jax.ShapeDtypeStruct(x.shape, f32), in_spe...  32 us
    unnamed x1, local copies, waits for them, and re-layouts  0.75 us

profile of v3, /device:TPU:2, one launch (start us, length us, event | category | flops | bytes accessed | tf_op | source)
XLA Modules:
  0.0 32.8 jit_solution(14617516069650301608)
XLA Ops:
  0.0 32.0 %shard_map.28 = f32[6,125,128]{2,1,0:T(8,128)S(1)} custom-call(f32[6,125,128]{2,1,0:T(8,128)} %bitcast.4, f32[6,1,128]{2,1,0:T(1,128)} %bitcast.5), custom_call_target="tpu_custom_call" | custom-call | tf_op jit(solution)/shard_map/pallas_call | solution.py:332
  32.0 0.7 %copy.4 = f32[125,6,128]{2,0,1:T(8,128)} copy(f32[125,6,128]{2,0,1:T(8,128)S(1)} %bitcast.3) | data formatting | bytes 768000

commit v4 on v3

--- a/solution.py
+++ b/solution.py
@@ -54,6 +54,8 @@
     out_ref,
     field,
     trans,
+    wide_up,
+    wide_down,
     halo_up,
     halo_down,
     vmag,
@@ -62,10 +64,15 @@
     parts_in,
     total,
     param,
+    param_up,
+    param_down,
+    scale_in,
     scale,
     load_sem,
     hs_sem,
     hr_sem,
+    ps_sem,
+    pr_sem,
     ms_sem,
     mr_sem,
 ):
@@ -85,7 +92,7 @@
         copy.start()
         loads.append(copy)
 
-    copy = pltpu.make_async_copy(cs_ref, scale, load_sem.at[LAYERS])
+    copy = pltpu.make_async_copy(cs_ref, scale_in, load_sem.at[LAYERS])
     copy.start()
     loads.append(copy)
 
@@ -126,6 +133,8 @@
     for k in range(LAYERS):
         weight[k] = jnp.where(which == layer(k), value, 0.0).astype(jnp.bfloat16)
 
+    param[...] = jnp.zeros_like(param)
+
     def edge(at_end):
         lane = lax.broadcasted_iota(jnp.int32, (1, 1, LANES), 2)
         return lax.rem(lane, NZ) == at_end * (NZ - 1)
@@ -153,22 +162,47 @@
         slice(low, min(low + 32, n_vel)) for low in range(0, n_vel, 32)
     ]
 
-    def send_layer(n, i):
-        src, dst, to = (
-            (LAYERS - 2, halo_up.at[n, 0], down_place),
-            (LAYERS - 1, halo_up.at[n, 1], down_place),
-            (0, halo_down.at[n], up_place),
-        )[i]
+    end = LAYERS - 1
+    halo_plan = (
+        (field.at[0, end], wide_up.at[3], down_place),
+        (field.at[0, end - 1], wide_up.at[2], down_place),
+        (field.at[0, 0], wide_down.at[0], up_place),
+        (field.at[0, pl.ds(end - 3, 2)], wide_up.at[pl.ds(0, 2)], down_place),
+        (field.at[0, 1], wide_down.at[1], up_place),
+        (field.at[2, end - 1], halo_up.at[1, 0], down_place),
+        (field.at[2, end], halo_up.at[1, 1], down_place),
+        (field.at[2, 0], halo_down.at[1], up_place),
+    )
+
+    def send(src, dst, to, send_sem, recv_sem):
         copy = pltpu.make_async_remote_copy(
-            src_ref=field.at[n, src],
+            src_ref=src,
             dst_ref=dst,
-            send_sem=hs_sem.at[n, i],
-            recv_sem=hr_sem.at[n, i],
+            send_sem=send_sem,
+            recv_sem=recv_sem,
             device_id={"space": to},
             device_id_type=MESH,
         )
         copy.start()
         return copy
+
+    def send_halo(i):
+        return send(*halo_plan[i], hs_sem.at[i], hr_sem.at[i])
+
+    def send_params():
+        return [
+            send(param.at[0], param_up, down_place, ps_sem.at[0], pr_sem.at[0]),
+            send(param.at[0], param_down, up_place, ps_sem.at[1], pr_sem.at[1]),
+        ]
+
+    def halo(n, rows):
+        if n == 0:
+            return wide_up[2, rows, :], wide_up[3, rows, :], wide_down[0, rows, :]
+        return (
+            halo_up[n - 1, 0, rows, :],
+            halo_up[n - 1, 1, rows, :],
+            halo_down[n - 1, rows, :],
+        )
 
     def moments_of(n, layers):
         acc = jnp.zeros((32, LANES), jnp.float32)
@@ -199,15 +233,18 @@
             copies.append(copy)
         return copies
 
+    def moved_yz(f, speed_y, speed_z):
+        g = f + half_slope(y_up(f), f, y_down(f))
+        change = speed_y * (g - y_up(g))
+        g = f + half_slope(z_up(f), f, z_down(f))
+        change = change + speed_z * (g - z_up(g))
+        return f - courant * change
+
     def transport_inside(n):
         for rows in chunks:
             f = field[n, :, rows, :]
             speed_x, speed_y, speed_z = vmag[0, rows, :], vmag[1, rows, :], vmag[2, rows, :]
-            g = f + half_slope(y_up(f), f, y_down(f))
-            change = speed_y * (g - y_up(g))
-            g = f + half_slope(z_up(f), f, z_down(f))
-            change = change + speed_z * (g - z_up(g))
-            t = f - courant * change
+            t = moved_yz(f, speed_y, speed_z)
             g = f[1:-1] + half_slope(f[:-2], f[1:-1], f[2:])
             moved = (courant * speed_x) * g
             trans[0, rows, :] = t[0]
@@ -225,10 +262,9 @@
     def finish_border(n):
         for rows in chunks:
             speed = courant * vmag[0, rows, :]
-            up2, up1 = halo_up[n, 0, rows, :], halo_up[n, 1, rows, :]
+            up2, up1, down = halo(n, rows)
             f0, f1 = field[n, 0, rows, :], field[n, 1, rows, :]
             f4, f5 = field[n, LAYERS - 2, rows, :], field[n, LAYERS - 1, rows, :]
-            down = halo_down[n, rows, :]
             into = speed * (up1 + half_slope(up2, up1, f0))
             first = speed * (f0 + half_slope(up1, f0, f1))
             last = speed * (f5 + half_slope(f4, f5, down))
@@ -255,49 +291,82 @@
         log_t = jnp.log(temper)
         rate = (
             (time_step * base_rate)
-            * param[5, :LAYERS, :]
+            * scale[:LAYERS, :]
             * density
             * jnp.exp((1.0 - visc_index) * log_t)
         )
-        param[0, :LAYERS, :] = sign_x.astype(jnp.float32) * flow_x
-        param[1, :LAYERS, :] = sign_y.astype(jnp.float32) * flow_y
-        param[2, :LAYERS, :] = sign_z.astype(jnp.float32) * flow_z
-        param[3, :LAYERS, :] = (-0.5 * LOG2E) / temper
-        param[4, :LAYERS, :] = rate * density * jnp.exp(-1.5 * log_t)
-        param[6, :LAYERS, :] = rate
-
-    def relaxed(n, k, rows):
-        f = field[n, k, rows, :]
-        p = [param[i, pl.ds(layer(k), 1), :] for i in range(7)]
+        param[n, 0, :LAYERS, :] = sign_x.astype(jnp.float32) * flow_x
+        param[n, 1, :LAYERS, :] = sign_y.astype(jnp.float32) * flow_y
+        param[n, 2, :LAYERS, :] = sign_z.astype(jnp.float32) * flow_z
+        param[n, 3, :LAYERS, :] = (-0.5 * LOG2E) / temper
+        param[n, 4, :LAYERS, :] = rate * density * jnp.exp(-1.5 * log_t)
+        param[n, 5, :LAYERS, :] = rate
+
+    def collided(f, moved, cells, k, rows):
+        p = [cells[i, pl.ds(layer(k), 1), :] for i in range(6)]
         dx = vmag[0, rows, :] - p[0]
         dy = vmag[1, rows, :] - p[1]
         dz = vmag[2, rows, :] - p[2]
         square = dx * dx + dy * dy + dz * dz
-        return trans[k, rows, :] + p[4] * jnp.exp2(square * p[3]) - p[6] * f
+        return moved + p[4] * jnp.exp2(square * p[3]) - p[5] * f
+
+    def relaxed(n, k, rows):
+        return collided(
+            field[n, k, rows, :], trans[k, rows, :], param.at[n], k, rows
+        )
+
+    def ghost_layers():
+        for rows in chunks:
+            speed = courant * vmag[0, rows, :]
+            up = [wide_up[i, rows, :] for i in range(4)]
+            first = field[0, 0, rows, :]
+            near = [field[0, end - 1, rows, :], field[0, end, rows, :]]
+            down = [wide_down[i, rows, :] for i in range(2)]
+            t = moved_yz(
+                jnp.stack([up[2], up[3], down[0]]), vmag[1, rows, :], vmag[2, rows, :]
+            )
+            g3 = up[1] + half_slope(up[0], up[1], up[2])
+            g2 = up[2] + half_slope(up[1], up[2], up[3])
+            g1 = up[3] + half_slope(up[2], up[3], first)
+            g5 = near[1] + half_slope(near[0], near[1], down[0])
+            g6 = down[0] + half_slope(near[1], down[0], down[1])
+            moved = (t[0] - speed * (g2 - g3), t[1] - speed * (g1 - g2), t[2] - speed * (g6 - g5))
+            halo_up[0, 0, rows, :] = collided(up[2], moved[0], param_up, end - 1, rows)
+            halo_up[0, 1, rows, :] = collided(up[3], moved[1], param_up, end, rows)
+            halo_down[0, rows, :] = collided(down[0], moved[2], param_down, 0, rows)
 
     for copy in loads:
         copy.wait()
     for k in range(LAYERS):
-        param[5, k : k + 1, :] = scale[k]
+        scale[k : k + 1, :] = scale_in[k]
     pl.semaphore_wait(barrier, n_oct + 1)
 
-    border = (0, 1, LAYERS - 1)
-    inside = tuple(range(2, LAYERS - 1))
-    halos = [send_layer(0, i) for i in (1, 0, 2)]
+    border = (0, 1, end)
+    inside = tuple(range(2, end))
+    halos = [send_halo(i) for i in (0, 1, 2)]
     moments = send_moments(0, moments_of(0, range(LAYERS)))
-    sent = halos + moments
+    extra = [send_halo(i) for i in (3, 4)]
+    sent = halos + moments + extra
     for n in range(STEPS):
         more = n < STEPS - 1
         transport_inside(n)
+        if n == 1:
+            for copy in extra:
+                copy.wait_recv()
+            ghost_layers()
         for copy in moments:
             copy.wait_recv()
         cell_params(n)
+        if n == 0:
+            params = send_params()
+            extra += params
+            sent += params
         early = []
         for k in reversed(inside):
             for rows in chunks:
                 put(n, k, rows, relaxed(n, k, rows))
-            if more and k == LAYERS - 2:
-                early.append(send_layer(n + 1, 0))
+            if n == 1 and k == end - 1:
+                early = [send_halo(5)]
         for k in border:
             for rows in chunks:
                 trans[k, rows, :] = relaxed(n, k, rows)
@@ -306,8 +375,10 @@
         for copy in halos:
             copy.wait_recv()
         finish_border(n)
+        halos = early
+        if n == 1:
+            halos = early + [send_halo(6), send_halo(7)]
         if more:
-            halos = early + [send_layer(n + 1, i) for i in (1, 2)]
             moments = send_moments(n + 1, acc + moments_of(n + 1, border))
             sent += halos + moments
     for copy in sent:
@@ -340,18 +411,25 @@
             scratch_shapes=[
                 pltpu.VMEM((STEPS, n_layers, n_vel, lanes), f32),
                 pltpu.VMEM((n_layers, n_vel, lanes), f32),
-                pltpu.VMEM((STEPS, 2, n_vel, lanes), f32),
-                pltpu.VMEM((STEPS, n_vel, lanes), f32),
+                pltpu.VMEM((4, n_vel, lanes), f32),
+                pltpu.VMEM((2, n_vel, lanes), f32),
+                pltpu.VMEM((2, 2, n_vel, lanes), f32),
+                pltpu.VMEM((2, n_vel, lanes), f32),
                 pltpu.VMEM((3, n_vel, lanes), f32),
                 pltpu.VMEM((n_layers, 32, n_vel), jnp.bfloat16),
                 pltpu.VMEM((STEPS, 32, lanes), f32),
                 pltpu.VMEM((STEPS, n_oct - 1, 32, lanes), f32),
                 pltpu.VMEM((32, lanes), f32),
-                pltpu.VMEM((7, 8, lanes), f32),
+                pltpu.VMEM((STEPS, 6, 8, lanes), f32),
+                pltpu.VMEM((6, 8, lanes), f32),
+                pltpu.VMEM((6, 8, lanes), f32),
                 pltpu.VMEM((n_layers, 1, lanes), f32),
+                pltpu.VMEM((8, lanes), f32),
                 dma((n_layers + 1,)),
-                dma((STEPS, 3)),
-                dma((STEPS, 3)),
+                dma((8,)),
+                dma((8,)),
+                dma((2,)),
+                dma((2,)),
                 dma((STEPS, n_oct - 1)),
                 dma((STEPS, n_oct - 1)),
             ],

time: 33 us -> 32.8 us (level)
  no operation moved by 1% of the time
where the time goes in v4:
time: 32.8 us; the launch traced here: 32.6 us
  Pallas kernels  31.9 us (97%)
  local copies, waits for them, and re-layouts  0.75 us (2%)
    pallas_call x1, Pallas kernels, per_device(): pl.pallas_call(body, out_shape=jax.ShapeDtypeStruct(x.shape, f32), in_spe...  31.9 us
    unnamed x1, local copies, waits for them, and re-layouts  0.75 us

profile of v4, /device:TPU:2, one launch (start us, length us, event | category | flops | bytes accessed | tf_op | source)
XLA Modules:
  0.0 32.6 jit_solution(5918963372417973256)
XLA Ops:
  0.0 31.9 %shard_map.28 = f32[6,125,128]{2,1,0:T(8,128)S(1)} custom-call(f32[6,125,128]{2,1,0:T(8,128)} %bitcast.4, f32[6,1,128]{2,1,0:T(1,128)} %bitcast.5), custom_call_target="tpu_custom_call" | custom-call | tf_op jit(solution)/shard_map/pallas_call | solution.py:403
  31.9 0.7 %copy.4 = f32[125,6,128]{2,0,1:T(8,128)} copy(f32[125,6,128]{2,0,1:T(8,128)S(1)} %bitcast.3) | data formatting | bytes 768000

commit v5 on v4

--- a/solution.py
+++ b/solution.py
@@ -345,11 +345,13 @@
     inside = tuple(range(2, end))
     halos = [send_halo(i) for i in (0, 1, 2)]
     moments = send_moments(0, moments_of(0, range(LAYERS)))
-    extra = [send_halo(i) for i in (3, 4)]
-    sent = halos + moments + extra
+    sent = halos + moments
     for n in range(STEPS):
         more = n < STEPS - 1
         transport_inside(n)
+        if n == 0:
+            extra = [send_halo(i) for i in (3, 4)]
+            sent += extra
         if n == 1:
             for copy in extra:
                 copy.wait_recv()

time: 32.8 us -> 32.3 us (0.985)
  Pallas kernels: 31.9 us -> 31.4 us
    pallas_call x1, Pallas kernels: 31.9 us -> 31.4 us  [per_device(): pl.pallas_call(body, out_shape=jax.ShapeDtypeStruct(x.shape, f32), in_spe...]
where the time goes in v5:
time: 32.3 us; the launch traced here: 32.1 us
  Pallas kernels  31.4 us (97%)
  local copies, waits for them, and re-layouts  0.75 us (2%)
    pallas_call x1, Pallas kernels, per_device(): pl.pallas_call(body, out_shape=jax.ShapeDtypeStruct(x.shape, f32), in_spe...  31.4 us
    unnamed x1, local copies, waits for them, and re-layouts  0.75 us

profile of v5, /device:TPU:2, one launch (start us, length us, event | category | flops | bytes accessed | tf_op | source)
XLA Modules:
  0.0 32.1 jit_solution(6335155692135172426)
XLA Ops:
  0.0 31.4 %shard_map.28 = f32[6,125,128]{2,1,0:T(8,128)S(1)} custom-call(f32[6,125,128]{2,1,0:T(8,128)} %bitcast.4, f32[6,1,128]{2,1,0:T(1,128)} %bitcast.5), custom_call_target="tpu_custom_call" | custom-call | tf_op jit(solution)/shard_map/pallas_call | solution.py:405
  31.4 0.7 %copy.4 = f32[125,6,128]{2,0,1:T(8,128)} copy(f32[125,6,128]{2,0,1:T(8,128)S(1)} %bitcast.3) | data formatting | bytes 768000

commit v6 on v5

--- a/solution.py
+++ b/solution.py
@@ -208,12 +208,12 @@
         acc = jnp.zeros((32, LANES), jnp.float32)
         for k in layers:
             rest = field[n, k]
-            for piece in range(3):
+            for piece in range(2):
                 term = rest.astype(jnp.bfloat16)
                 acc = acc + jnp.dot(
                     weight[k], term, preferred_element_type=jnp.float32
                 )
-                if piece < 2:
+                if piece < 1:
                     rest = rest - term.astype(jnp.float32)
         return acc
 
@@ -259,15 +259,26 @@
         else:
             out_ref[layer(k), rows, :] = new
 
+    def border_fluxes(n, rows):
+        speed = courant * vmag[0, rows, :]
+        up2, up1, down = halo(n, rows)
+        f0, f1 = field[n, 0, rows, :], field[n, 1, rows, :]
+        f4, f5 = field[n, LAYERS - 2, rows, :], field[n, LAYERS - 1, rows, :]
+        into = speed * (up1 + half_slope(up2, up1, f0))
+        first = speed * (f0 + half_slope(up1, f0, f1))
+        last = speed * (f5 + half_slope(f4, f5, down))
+        return into, first, last
+
+    def transport_border(n):
+        for rows in chunks:
+            into, first, last = border_fluxes(n, rows)
+            trans[0, rows, :] = trans[0, rows, :] + (into - first)
+            trans[1, rows, :] = trans[1, rows, :] + first
+            trans[LAYERS - 1, rows, :] = trans[LAYERS - 1, rows, :] - last
+
     def finish_border(n):
         for rows in chunks:
-            speed = courant * vmag[0, rows, :]
-            up2, up1, down = halo(n, rows)
-            f0, f1 = field[n, 0, rows, :], field[n, 1, rows, :]
-            f4, f5 = field[n, LAYERS - 2, rows, :], field[n, LAYERS - 1, rows, :]
-            into = speed * (up1 + half_slope(up2, up1, f0))
-            first = speed * (f0 + half_slope(up1, f0, f1))
-            last = speed * (f5 + half_slope(f4, f5, down))
+            into, first, last = border_fluxes(n, rows)
             put(n, LAYERS - 1, rows, trans[LAYERS - 1, rows, :] - last)
             put(n, 0, rows, trans[0, rows, :] + (into - first))
             put(n, 1, rows, trans[1, rows, :] + first)
@@ -356,6 +367,7 @@
             for copy in extra:
                 copy.wait_recv()
             ghost_layers()
+            transport_border(n)
         for copy in moments:
             copy.wait_recv()
         cell_params(n)
@@ -363,12 +375,21 @@
             params = send_params()
             extra += params
             sent += params
-        early = []
-        for k in reversed(inside):
+        if n == 1:
+            halos = []
+            for k, i in ((end, 6), (end - 1, 5), (0, 7)):
+                for rows in chunks:
+                    put(n, k, rows, relaxed(n, k, rows))
+                halos.append(send_halo(i))
+            for k in range(1, end - 1):
+                for rows in chunks:
+                    put(n, k, rows, relaxed(n, k, rows))
+            moments = send_moments(n + 1, moments_of(n + 1, range(LAYERS)))
+            sent += halos + moments
+            continue
+        for k in inside:
             for rows in chunks:
                 put(n, k, rows, relaxed(n, k, rows))
-            if n == 1 and k == end - 1:
-                early = [send_halo(5)]
         for k in border:
             for rows in chunks:
                 trans[k, rows, :] = relaxed(n, k, rows)
@@ -377,12 +398,9 @@
         for copy in halos:
             copy.wait_recv()
         finish_border(n)
-        halos = early
-        if n == 1:
-            halos = early + [send_halo(6), send_halo(7)]
         if more:
             moments = send_moments(n + 1, acc + moments_of(n + 1, border))
-            sent += halos + moments
+            sent += moments
     for copy in sent:
         copy.wait_send()
 

time: 32.3 us -> 32.1 us (level)
  no operation moved by 1% of the time
where the time goes in v6:
time: 32.1 us; the launch traced here: 32 us
  Pallas kernels  31.2 us (97%)
  local copies, waits for them, and re-layouts  0.75 us (2%)
    pallas_call x1, Pallas kernels, per_device(): pl.pallas_call(body, out_shape=jax.ShapeDtypeStruct(x.shape, f32), in_spe...  31.2 us
    unnamed x1, local copies, waits for them, and re-layouts  0.75 us

profile of v6, /device:TPU:2, one launch (start us, length us, event | category | flops | bytes accessed | tf_op | source)
XLA Modules:
  0.0 32.0 jit_solution(15575888954730674605)
XLA Ops:
  0.0 31.2 %shard_map.28 = f32[6,125,128]{2,1,0:T(8,128)S(1)} custom-call(f32[6,125,128]{2,1,0:T(8,128)} %bitcast.4, f32[6,1,128]{2,1,0:T(1,128)} %bitcast.5), custom_call_target="tpu_custom_call" | custom-call | tf_op jit(solution)/shard_map/pallas_call | solution.py:423
  31.2 0.7 %copy.4 = f32[125,6,128]{2,0,1:T(8,128)} copy(f32[125,6,128]{2,0,1:T(8,128)S(1)} %bitcast.3) | data formatting | bytes 768000
